TPU v7x, 256 devices: a whole 4x4x8 slice. The times are simulated.
256 devices in a mesh: prow: 16 (over z, core), pcol: 16 (over x, y).
Axes of the slice: x: 4, y: 4, z: 8, core: 2. Of those that a mesh axis runs over, the one named last changes fastest.
Arguments:
- inv_lead: float32 [4, 16, 256, 4, 16, 256], P(None, 'prow', None, None, 'pcol'), may hold values from -1 to 2, as said below
- h_lead: float32 [4, 16, 256, 6, 16, 256], P(None, 'pcol', None, None, 'prow'), may hold values from -6 to 6
- h_slab: float32 [512, 6, 16, 256], P('pcol', None, 'prow'), may hold values from -6 to 6
- l_panel: float32 [512, 4, 16, 256], P('pcol', None, 'prow'), may hold values from -0.046875 to 0.046875
- l_diag: float32 [512, 512], replicated, may hold values from -1 to 2, as said below
Outputs:
- x_slab: float32 [512, 6, 16, 256], P('pcol', None, 'prow')
- y_lead: float32 [512, 4, 16, 256], P('pcol', None, 'prow')
- y_diag: float32 [512, 512], P('pcol', 'prow')
Inputs may be any that keep to these rules, and one draw needn't show every extreme that they name: inv_lead is lower triangular in natural order, with diagonal entries between 1 and 2. l_diag is lower triangular, with diagonal entries between 1 and 2.
All inputs are finite; a program needn't handle non-finite values.
Results may differ from a plain program's by a relative error of at most 0.00018.
Values sent between devices are 32-bit elements; how exact they have to be, the bound alone decides.
No kernel may reach another device: no remote copies, remote signals or barrier semaphores. Data moves between devices by JAX's collectives and lax.ppermute only.
A program may use at most 128 MiB of HBM per device.

v0:
```python
import jax
import jax.numpy as jnp
from jax import lax
from jax.sharding import PartitionSpec as P


def copy_for_each(value, axis):
    copies = jnp.broadcast_to(value, (lax.axis_size(axis), *value.shape))
    return lax.all_to_all(copies, axis, split_axis=0, concat_axis=0, tiled=True)


def joined_along(parts, dim):
    lengths = list(parts.shape[1:])
    lengths[dim] *= parts.shape[0]
    return jnp.moveaxis(parts, 0, dim).reshape(lengths)


def gathered_copies(value, axis, dim):
    parts = copy_for_each(value, axis)
    return joined_along(parts, dim)


def in_blocks(value, dim, size):
    lengths = value.shape
    parts = value.reshape(*lengths[:dim], size, lengths[dim] // size, *lengths[dim + 1 :])
    return jnp.moveaxis(parts, dim, 0)


def sum_at_owner(value, axis, dim):
    parts = in_blocks(value, dim, lax.axis_size(axis))
    arrived = lax.all_to_all(parts, axis, split_axis=0, concat_axis=0, tiled=True)
    return arrived.sum(axis=0)


def in_one_piece(arrays, axis, dim, along):
    widths = [a.shape[along] for a in arrays]
    both = jnp.concatenate(arrays, axis=along)
    result = lax.psum_scatter(both, axis, scatter_dimension=dim, tiled=True)
    return tuple(jnp.split(result, [sum(widths[:k]) for k in range(1, len(widths))], axis=along))


def matmul_hi(left, right):
    return jnp.dot(left, right, precision=lax.Precision.HIGHEST, preferred_element_type=jnp.float32)


def matmul_trans(left, right):
    return lax.dot_general(
        left,
        right,
        (((1,), (1,)), ((), ())),
        precision=lax.Precision.HIGHEST,
        preferred_element_type=jnp.float32,
    )


def invert_diag(l_diag, block_size):
    diag_top = l_diag[:block_size, :block_size]
    diag_bottom = l_diag[block_size:, block_size:]
    off_block = l_diag[block_size:, :block_size]
    identity = jnp.eye(block_size, dtype=jnp.float32)
    top_inv = lax.linalg.triangular_solve(diag_top, identity, left_side=True, lower=True)
    bottom_inv = lax.linalg.triangular_solve(diag_bottom, identity, left_side=True, lower=True)
    corner = -matmul_hi(bottom_inv, matmul_hi(off_block, top_inv))
    upper_rows = jnp.concatenate([top_inv, jnp.zeros_like(top_inv)], axis=1)
    lower_rows = jnp.concatenate([corner, bottom_inv], axis=1)
    return jnp.concatenate([upper_rows, lower_rows], axis=0)


def per_device(inv_lead, h_lead, h_slab, l_panel, l_diag):
    slab_rows = l_diag.shape[0]
    block_size = l_panel.shape[3]
    prev_blocks = l_panel.shape[1]
    x_rows = l_panel.shape[0]
    h_blocks = h_slab.shape[1]
    diag_inv = invert_diag(l_diag, slab_rows // 2)
    inv_local = inv_lead.reshape(prev_blocks * block_size, -1)
    col_width = inv_local.shape[1]
    col_blocks = col_width // block_size
    h_local = h_lead.reshape(col_width, -1)
    h_side = h_slab.reshape(x_rows, -1)
    y_rows = slab_rows // lax.axis_size("prow")
    row_start = lax.axis_index("prow") * y_rows
    col_start = lax.axis_index("pcol") * x_rows
    piece = gathered_copies(l_panel, "pcol", 0)
    factor = matmul_hi(diag_inv, piece.reshape(piece.shape[0], -1))
    side_term = matmul_hi(lax.dynamic_slice_in_dim(diag_inv, col_start, x_rows, 1), h_side)
    own_panel = sum_at_owner(-matmul_hi(factor, inv_local), "prow", 0)
    product = matmul_hi(lax.all_gather(own_panel, "prow", axis=0, tiled=True), h_local)
    x_local = sum_at_owner(product + side_term, "pcol", 0)
    x_slab = x_local.reshape(x_rows, h_blocks, 1, block_size)
    kept_cols = x_slab[:, : prev_blocks + 1]
    widened = lax.all_gather(kept_cols, "prow", axis=2, tiled=True).reshape(x_rows, -1)
    prev_rows = prev_blocks * block_size * lax.axis_size("prow")
    head_cols = widened[:, :prev_rows]
    tail_cols = widened[:, prev_rows : prev_rows + slab_rows]
    shifted_x = lax.all_to_all(
        head_cols.reshape(x_rows, col_blocks, lax.axis_size("pcol"), block_size),
        "pcol",
        split_axis=2,
        concat_axis=0,
        tiled=True,
    )
    shifted_x = shifted_x.reshape(slab_rows, col_width)
    lead_part = matmul_trans(shifted_x, inv_local)
    diag_part = matmul_trans(shifted_x, own_panel)
    y_first, y_block = in_one_piece((lead_part, diag_part), "pcol", 0, 1)
    diag_rows = lax.dynamic_slice_in_dim(diag_inv, row_start, y_rows, 0)
    y_diag = y_block + matmul_trans(tail_cols, diag_rows)
    return (x_slab, y_first.reshape(x_rows, prev_blocks, 1, block_size), y_diag)


def solution(mesh):
    return jax.shard_map(
        per_device,
        mesh=mesh,
        in_specs=(
            P(None, "prow", None, None, "pcol", None),
            P(None, "pcol", None, None, "prow", None),
            P("pcol", None, "prow", None),
            P("pcol", None, "prow", None),
            P(),
        ),
        out_specs=(P("pcol", None, "prow", None), P("pcol", None, "prow", None), P("pcol", "prow")),
        check_vma=False,
    )
```

profile of v0, /device:TPU:2, one launch (start us, length us, event | category | flops | bytes accessed | tf_op | source)
XLA Modules:
  0.0 457.1 jit_solution(1383191247335577584)
XLA Ops:
  7.2 0.9 copy.41
  8.1 2.9 broadcast_in_dim.4
  11.1 7.5 %all-to-all-start = ((f32[16,32,4,1,256]{4,3,2,1,0:T(1,128)}), f32[16,32,4,1,256]{4,3,2,1,0:T(1,128)S(1)}, u32[]{:S(2)}, u32[]{:S(2)}) async-start(f32[16,32,4,1,256]{4,3,2,1,0:T(1,128)} %broadcast_in_dim.4), calls=%async_computation | async-start | bytes 4194304 | tf_op jit(solution)/shard_map/all_to_all | solution.py:9
  18.6 1.1 fusion.3
  19.8 3.8 while.4
  19.8 0.6 fusion.45
  20.4 1.3 bitcast_dynamic-update-slice_fusion.4
  21.7 0.6 fusion.45
  22.3 1.3 bitcast_dynamic-update-slice_fusion.4
  23.6 19.7 %custom-call.4 = f32[2,128,128]{1,2,0:T(8,128)S(1)} custom-call(f32[2,128,128]{2,1,0:T(8,128)S(1)} %get-tuple-element.18), custom_call_target="InvertDiagBlocksLowerTriangular" | custom-call | tf_op jit(solution)/shard_map/triangular_solve/custom-call.1 | solution.py:61
  43.3 4.0 while.5
  43.3 0.6 fusion.46
  43.9 1.4 bitcast_dynamic-update-slice_fusion.5
  45.3 0.6 fusion.46
  45.9 1.4 bitcast_dynamic-update-slice_fusion.5
  47.3 19.7 %custom-call.5 = f32[2,128,128]{1,2,0:T(8,128)S(1)} custom-call(f32[2,128,128]{2,1,0:T(8,128)S(1)} %get-tuple-element.19), custom_call_target="InvertDiagBlocksLowerTriangular" | custom-call | tf_op jit(solution)/shard_map/triangular_solve/custom-call.1 | solution.py:62
  67.0 14.2 %reduce.1 = f32[4,256,4,256]{3,2,1,0:T(4,128)} reduce(f32[4,1,256,4,1,256]{5,4,3,2,1,0:T(1,128)} %param.7, f32[]{:T(128)} %constant.47), dimensions={1,4}, to_apply=%param.7.reduce_sub_computation | reduce | bytes 8388612 | tf_op args[0]
  81.2 5.2 %copy.34 = f32[128,8,4,256]{3,1,2,0:T(8,128)} copy(f32[128,8,4,256]{3,2,1,0:T(4,128)} %bitcast.82) | data formatting | bytes 8388608
  88.2 1.5 fusion.6
  90.2 7.4 %reduce = f32[16,32,4,256]{3,2,1,0:T(4,128)} reduce(f32[16,32,4,1,256]{4,3,2,1,0:T(1,128)S(1)} %all-to-all-done, f32[]{:T(128)} %constant.47), dimensions={3}, to_apply=%all_to_all.20.reduce_sub_computation | reduce | bytes 4194308 | tf_op jit(solution)/shard_map/all_to_all | solution.py:9
  97.6 2.1 copy.33
  99.7 4.0 fusion.22
  103.7 6.9 %convolution_negate_fusion = f32[512,1024]{1,0:T(8,128)S(1)} fusion(f32[512,1024]{1,0:T(8,128)S(1)} %fusion.22, f32[1024,1024]{1,0:T(8,128)S(1)} %bitcast.77), kind=kOutput, calls=%fused_computation.6 | convolution fusion | flops 6442975232 | bytes 8388608 | tf_op jit(solution)/shard_map/dot_general | solution.py:43
  110.6 58.0 %all_to_all.31 = f32[16,32,1024]{2,1,0:T(8,128)S(1)} all-to-all(f32[16,32,1024]{2,1,0:T(8,128)S(1)} %bitcast.92), channel_id=1, replica_groups=mesh['prow'=16,'pcol'=16] {'prow'}, dimensions={0} | all-to-all | bytes 4194304 | tf_op jit(solution)/shard_map/all_to_all | solution.py:31
  168.6 0.8 reduce_sum.18
  169.5 37.4 %reduce.2 = f32[4,256,6,256]{3,2,1,0:T(8,128)} reduce(f32[4,1,256,6,1,256]{5,4,3,2,1,0:T(1,128)} %param.8, f32[]{:T(128)} %constant.47), dimensions={1,4}, to_apply=%param.8.reduce_sub_computation | reduce | bytes 12582916 | tf_op args[1]
  206.8 9.2 %copy.35 = f32[128,8,6,256]{3,1,2,0:T(8,128)} copy(f32[128,8,6,256]{3,2,1,0:T(8,128)} %bitcast.79) | data formatting | bytes 12582912
  216.1 0.5 reduce.3
  216.8 13.7 %fusion.25 = f32[512,1536]{1,0:T(8,128)S(1)} fusion(f32[512,1024]{1,0:T(8,128)} %all-gather.3.cloned.1.call-done, f32[1024,1536]{1,0:T(8,128)} %bitcast.93), kind=kOutput, calls=%fused_computation.47 | convolution fusion | flops 9663676416 | bytes 11534336 | tf_op jit(solution)/shard_map/dot_general | solution.py:43
  230.4 2.8 convolution_add_fusion
  233.2 45.1 %all_to_all.32 = f32[16,32,1536]{2,1,0:T(8,128)S(1)} all-to-all(f32[16,32,1536]{2,1,0:T(8,128)S(1)} %bitcast.83), channel_id=1, replica_groups=mesh['prow'=16,'pcol'=16] {'pcol'}, dimensions={0} | all-to-all | bytes 6291456 | tf_op jit(solution)/shard_map/all_to_all | solution.py:31
  278.6 0.7 copy.24
  279.4 36.6 %all-gather.5.cloned.1.call-done = f32[32,5,16,256]{3,0,1,2:T(8,128)} async-done(((f32[32,5,1,256]{3,0,1,2:T(8,128)}), f32[32,5,16,256]{3,0,1,2:T(8,128)}) %all-gather.5.cloned.1.call-update) | async-done | bytes 2621456 | tf_op jit(solution)/shard_map/all_gather | solution.py:92
  315.9 3.3 copy.25
  319.2 1.5 copy.37
  320.9 0.6 copy.38
  321.5 1.4 copy.26
  322.9 33.8 %all_to_all.30 = f32[32,4,16,256]{3,1,0,2:T(4,128)S(1)} all-to-all(f32[32,4,16,256]{3,1,0,2:T(4,128)S(1)} %copy.26), channel_id=1, replica_groups=mesh['prow'=16,'pcol'=16] {'pcol'}, dimensions={2} | all-to-all | bytes 4194304 | tf_op jit(solution)/shard_map/all_to_all | solution.py:96
  356.7 0.5 copy.39
  357.1 1.7 copy-done.1
  358.8 7.0 %fusion.26 = f32[512,1024]{1,0:T(8,128)S(1)} fusion(f32[512,1024]{1,0:T(8,128)S(1)} %bitcast.80, f32[1024,1024]{1,0:T(8,128)S(1)} %bitcast.78), kind=kOutput, calls=%fused_computation.48 | convolution fusion | flops 6442450944 | bytes 8388608 | tf_op jit(solution)/shard_map/dot_general | solution.py:47
  365.8 1.8 fusion.27
  367.6 1.6 pad_maximum_fusion
  369.2 0.9 copy.28
  370.1 76.6 %reduce-scatter.2.cloned.1.call-done = f32[32,1056]{1,0:T(8,128)} async-done(((f32[512,1056]{1,0:T(8,128)}), f32[32,1056]{1,0:T(8,128)}) %reduce-scatter.2.cloned.1.call-update) | async-done | bytes 135184 | tf_op jit(solution)/shard_map/reduce_scatter | solution.py:38
  446.7 0.9 split.8
  447.6 0.8 reshape.82
  448.5 1.6 convolution_add_fusion.1
  (39 shorter events, 3.1 us)
Async XLA Ops:
  11.1 79.2 %all-to-all-start = ((f32[16,32,4,1,256]{4,3,2,1,0:T(1,128)}), f32[16,32,4,1,256]{4,3,2,1,0:T(1,128)S(1)}, u32[]{:S(2)}, u32[]{:S(2)}) async-start(f32[16,32,4,1,256]{4,3,2,1,0:T(1,128)} %broadcast_in_dim.4), calls=%async_computation | async-start | bytes 4194304 | tf_op jit(solution)/shard_map/all_to_all | solution.py:9
  18.5 198.2 %all-gather.3.cloned.1.call-start = ((), (), s32[]{:S(2)}) async-start(), calls=%async_computation.5 | async-start | bytes 2228224 | tf_op jit(solution)/shard_map/all_gather | solution.py:88
  99.7 4.0 copy-start
  169.4 146.5 %all-gather.5.cloned.1.call-start = ((), (), s32[]{:S(2)}) async-start(), calls=%async_computation.6 | async-start | bytes 2785280 | tf_op jit(solution)/shard_map/all_gather | solution.py:92
  206.8 9.2 %copy-start.4 = (f32[32,6,1,256]{3,2,1,0:T(1,128)S(1)}, f32[32,6,1,256]{3,2,1,0:T(1,128)}, u32[]{:S(2)}) copy-start(f32[32,6,1,256]{3,2,1,0:T(1,128)} %param.9) | copy-start | bytes 589828
  216.7 13.7 %copy-start.2 = (f32[512,512]{1,0:T(8,128)}, f32[512,512]{1,0:T(8,128)S(1)}, u32[]{:S(2)}) copy-start(f32[512,512]{1,0:T(8,128)S(1)} %select_maximum_fusion) | copy-start | bytes 3145732
  279.3 167.4 %reduce-scatter.2.cloned.1.call-start = ((), (), s32[]{:S(2)}) async-start(), calls=%async_computation.7 | async-start | bytes 2506752 | tf_op jit(solution)/shard_map/reduce_scatter | solution.py:38
  356.7 2.2 copy-start.1
  358.8 7.0 %copy-start.3 = (f32[32,1024]{1,0:T(8,128)S(1)}, f32[32,1024]{1,0:T(8,128)}, u32[]{:S(2)}) copy-start(f32[32,1024]{1,0:T(8,128)} %reduce_sum.18) | copy-start | bytes 393220
Sparse Core Ops, SparseCore 0:
  169.5 37.7 all-gather.2
  279.4 36.4 all-gather.4
  369.4 77.3 reduce-scatter.1
where the time goes:
time: 464 us; the launch traced here: 457 us
  blocking collectives  137 us (30%)
  waiting for transfers between devices  113 us (24%)
  other arithmetic  103 us (22%)
  matrix products  41.4 us (9%)
  local copies, waits for them, and re-layouts  40.7 us (9%)
  between operations  14.5 us (3%)
  starting transfers between devices  7.6 us (2%)
    all_to_all x2, blocking collectives, sum_at_owner(): lax.all_to_all(parts, axis, split_axis=0, concat_axis=0, tiled=True)  103 us
    reduce_scatter x1, waiting for transfers between devices, in_one_piece(): result = lax.psum_scatter(both, axis, scatter_dimension=dim, tiled=True)  76.6 us
    unnamed x3, other arithmetic  52.1 us
    all_gather x1, waiting for transfers between devices, per_device(): lax.all_gather(kept_cols, 'prow', axis=2, tiled=True).reshape(x_rows, -1)  36.6 us
    all_to_all x1, blocking collectives, per_device(): lax.all_to_all(head_cols.reshape(x_rows, col_blocks, lax.axis_size('pcol'...  33.8 us
    dot_general x6, matrix products, matmul_hi(): jnp.dot(left, right, precision=lax.Precision.HIGHEST, preferred_element_t...  29.3 us
    unnamed x19, local copies, waits for them, and re-layouts  22.7 us
    another operation x2, other arithmetic, invert_diag(): lax.linalg.triangular_solve(diag_bottom, identity, left_side=True, lower=...  20.7 us
  transfers between devices with their start and end apart: 4, of which 2 were waited for; matrix products, arithmetic and copies ran while one was open for 26% of the time, Pallas kernels for 0%

commit v1 on v0

--- a/solution.py
+++ b/solution.py
@@ -93,13 +93,11 @@
     prev_rows = prev_blocks * block_size * lax.axis_size("prow")
     head_cols = widened[:, :prev_rows]
     tail_cols = widened[:, prev_rows : prev_rows + slab_rows]
-    shifted_x = lax.all_to_all(
-        head_cols.reshape(x_rows, col_blocks, lax.axis_size("pcol"), block_size),
-        "pcol",
-        split_axis=2,
-        concat_axis=0,
-        tiled=True,
-    )
+    x = head_cols.reshape(x_rows, col_blocks, lax.axis_size("pcol"), block_size)
+    count = lax.axis_size("pcol")
+    tiles = jnp.stack(jnp.split(x, count, axis=2), axis=0)
+    tiles = lax.all_to_all(tiles, "pcol", split_axis=0, concat_axis=0)
+    shifted_x = jnp.concatenate(tiles, axis=0)
     shifted_x = shifted_x.reshape(slab_rows, col_width)
     lead_part = matmul_trans(shifted_x, inv_local)
     diag_part = matmul_trans(shifted_x, own_panel)

time: 464 us -> 474 us (1.022)
  other arithmetic: 103 us -> 111 us
    all_to_all x0 -> x1, other arithmetic: none -> 8.43 us  [per_device(): tiles = lax.all_to_all(tiles, 'pcol', split_axis=0, concat_axis=0)]
    unnamed x19 -> x34, local copies, waits for them, and re-layouts: 22.7 us -> 25.4 us
where the time goes in v1:
time: 474 us; the launch traced here: 467 us
  blocking collectives  137 us (29%)
  waiting for transfers between devices  113 us (24%)
  other arithmetic  111 us (23%)
  local copies, waits for them, and re-layouts  42.5 us (9%)
  matrix products  41.7 us (9%)
  between operations  14.3 us (3%)
  starting transfers between devices  7.6 us (2%)
    all_to_all x2, blocking collectives, sum_at_owner(): lax.all_to_all(parts, axis, split_axis=0, concat_axis=0, tiled=True)  103 us
    reduce_scatter x1, waiting for transfers between devices, in_one_piece(): result = lax.psum_scatter(both, axis, scatter_dimension=dim, tiled=True)  76.6 us
    unnamed x3, other arithmetic  52.1 us
    all_gather x1, waiting for transfers between devices, per_device(): lax.all_gather(kept_cols, 'prow', axis=2, tiled=True).reshape(x_rows, -1)  36.6 us
    all_to_all x1, blocking collectives, per_device(): tiles = lax.all_to_all(tiles, 'pcol', split_axis=0, concat_axis=0)  33.6 us
    dot_general x6, matrix products, matmul_hi(): jnp.dot(left, right, precision=lax.Precision.HIGHEST, preferred_element_t...  29.4 us
    unnamed x34, local copies, waits for them, and re-layouts  25.4 us
    another operation x2, other arithmetic, invert_diag(): lax.linalg.triangular_solve(diag_bottom, identity, left_side=True, lower=...  20.7 us
  transfers between devices with their start and end apart: 4, of which 2 were waited for; matrix products, arithmetic and copies ran while one was open for 26% of the time, Pallas kernels for 0%

profile of v1, /device:TPU:2, one launch (start us, length us, event | category | flops | bytes accessed | tf_op | source)
XLA Modules:
  0.0 467.4 jit_solution(13552269376336275357)
XLA Ops:
  7.2 0.9 copy.32
  8.1 2.9 broadcast_in_dim.4
  11.1 7.5 %all-to-all-start = ((f32[16,32,4,1,256]{4,3,2,1,0:T(1,128)}), f32[16,32,4,1,256]{4,3,2,1,0:T(1,128)S(1)}, u32[]{:S(2)}, u32[]{:S(2)}) async-start(f32[16,32,4,1,256]{4,3,2,1,0:T(1,128)} %broadcast_in_dim.4), calls=%async_computation | async-start | bytes 4194304 | tf_op jit(solution)/shard_map/all_to_all | solution.py:9
  18.6 1.1 fusion.3
  19.8 4.1 while.4
  19.8 0.6 fusion.61
  20.4 1.4 bitcast_dynamic-update-slice_fusion.4
  21.9 0.6 fusion.61
  22.4 1.4 bitcast_dynamic-update-slice_fusion.4
  23.9 19.7 %custom-call.4 = f32[2,128,128]{1,2,0:T(8,128)S(1)} custom-call(f32[2,128,128]{2,1,0:T(8,128)S(1)} %get-tuple-element.18), custom_call_target="InvertDiagBlocksLowerTriangular" | custom-call | tf_op jit(solution)/shard_map/triangular_solve/custom-call.1 | solution.py:61
  43.6 4.0 while.5
  43.6 0.6 fusion.62
  44.2 1.4 bitcast_dynamic-update-slice_fusion.5
  45.6 0.6 fusion.62
  46.2 1.4 bitcast_dynamic-update-slice_fusion.5
  47.6 19.7 %custom-call.5 = f32[2,128,128]{1,2,0:T(8,128)S(1)} custom-call(f32[2,128,128]{2,1,0:T(8,128)S(1)} %get-tuple-element.19), custom_call_target="InvertDiagBlocksLowerTriangular" | custom-call | tf_op jit(solution)/shard_map/triangular_solve/custom-call.1 | solution.py:62
  67.3 14.3 %reduce.1 = f32[4,256,4,256]{3,2,1,0:T(4,128)} reduce(f32[4,1,256,4,1,256]{5,4,3,2,1,0:T(1,128)} %param.7, f32[]{:T(128)} %constant.47), dimensions={1,4}, to_apply=%param.7.reduce_sub_computation | reduce | bytes 8388612 | tf_op args[0]
  81.6 5.2 %copy.25 = f32[128,8,4,256]{3,1,2,0:T(8,128)} copy(f32[128,8,4,256]{3,2,1,0:T(4,128)} %bitcast.142) | data formatting | bytes 8388608
  88.6 1.5 fusion.6
  90.6 7.4 %reduce = f32[16,32,4,256]{3,2,1,0:T(4,128)} reduce(f32[16,32,4,1,256]{4,3,2,1,0:T(1,128)S(1)} %all-to-all-done, f32[]{:T(128)} %constant.47), dimensions={3}, to_apply=%all_to_all.12.reduce_sub_computation | reduce | bytes 4194308 | tf_op jit(solution)/shard_map/all_to_all | solution.py:9
  98.0 2.1 copy.24
  100.0 4.1 fusion.38
  104.1 6.9 %convolution_negate_fusion = f32[512,1024]{1,0:T(8,128)S(1)} fusion(f32[512,1024]{1,0:T(8,128)S(1)} %fusion.38, f32[1024,1024]{1,0:T(8,128)S(1)} %bitcast.137), kind=kOutput, calls=%fused_computation.6 | convolution fusion | flops 6442975232 | bytes 8388608 | tf_op jit(solution)/shard_map/dot_general | solution.py:43
  111.1 58.0 %all_to_all.21 = f32[16,32,1024]{2,1,0:T(8,128)S(1)} all-to-all(f32[16,32,1024]{2,1,0:T(8,128)S(1)} %bitcast.167), channel_id=1, replica_groups=mesh['prow'=16,'pcol'=16] {'prow'}, dimensions={0} | all-to-all | bytes 4194304 | tf_op jit(solution)/shard_map/all_to_all | solution.py:31
  169.1 0.8 reduce_sum.18
  169.9 37.4 %reduce.2 = f32[4,256,6,256]{3,2,1,0:T(8,128)} reduce(f32[4,1,256,6,1,256]{5,4,3,2,1,0:T(1,128)} %param.8, f32[]{:T(128)} %constant.47), dimensions={1,4}, to_apply=%param.8.reduce_sub_computation | reduce | bytes 12582916 | tf_op args[1]
  207.3 9.2 %copy.26 = f32[128,8,6,256]{3,1,2,0:T(8,128)} copy(f32[128,8,6,256]{3,2,1,0:T(8,128)} %bitcast.139) | data formatting | bytes 12582912
  216.5 0.5 reduce.3
  217.2 13.7 %fusion.41 = f32[512,1536]{1,0:T(8,128)S(1)} fusion(f32[512,1024]{1,0:T(8,128)} %all-gather.3.cloned.1.call-done, f32[1024,1536]{1,0:T(8,128)} %bitcast.168), kind=kOutput, calls=%fused_computation.79 | convolution fusion | flops 9663676416 | bytes 11534336 | tf_op jit(solution)/shard_map/dot_general | solution.py:43
  230.9 2.8 convolution_add_fusion
  233.7 45.1 %all_to_all.22 = f32[16,32,1536]{2,1,0:T(8,128)S(1)} all-to-all(f32[16,32,1536]{2,1,0:T(8,128)S(1)} %bitcast.143), channel_id=1, replica_groups=mesh['prow'=16,'pcol'=16] {'pcol'}, dimensions={0} | all-to-all | bytes 6291456 | tf_op jit(solution)/shard_map/all_to_all | solution.py:31
  279.0 0.7 copy.16
  279.8 36.6 %all-gather.5.cloned.1.call-done = f32[32,5,16,256]{3,0,1,2:T(8,128)} async-done(((f32[32,5,1,256]{3,0,1,2:T(8,128)}), f32[32,5,16,256]{3,0,1,2:T(8,128)}) %all-gather.5.cloned.1.call-update) | async-done | bytes 2621456 | tf_op jit(solution)/shard_map/all_gather | solution.py:92
  316.4 3.3 copy.17
  319.7 1.5 copy.28
  321.3 0.6 copy.29
  324.3 33.6 %all_to_all.20 = f32[16,32,4,1,256]{4,3,2,1,0:T(1,128)} all-to-all(f32[16,32,4,1,256]{4,3,2,1,0:T(1,128)S(1)} %fusion.9), channel_id=1, replica_groups=mesh['prow'=16,'pcol'=16] {'pcol'}, dimensions={0} | all-to-all | bytes 4194304 | tf_op jit(solution)/shard_map/all_to_all | solution.py:99
  358.0 8.4 %reduce.4 = f32[16,32,4,256]{3,2,1,0:T(4,128)} reduce(f32[16,32,4,1,256]{4,3,2,1,0:T(1,128)} %all_to_all.20, f32[]{:T(128)} %constant.47), dimensions={3}, to_apply=%all_to_all.15.reduce_sub_computation | reduce | bytes 4194308 | tf_op jit(solution)/shard_map/all_to_all | solution.py:99
  366.4 2.2 copy.30
  368.6 0.6 copy-done.1
  369.2 7.2 %fusion.42 = f32[512,1024]{1,0:T(8,128)S(1)} fusion(f32[512,1024]{1,0:T(8,128)S(1)} %bitcast.140, f32[1024,1024]{1,0:T(8,128)S(1)} %bitcast.138), kind=kOutput, calls=%fused_computation.80 | convolution fusion | flops 6442450944 | bytes 8388608 | tf_op jit(solution)/shard_map/dot_general | solution.py:47
  376.4 1.8 fusion.43
  378.1 1.6 pad_maximum_fusion
  379.8 0.9 copy.19
  380.7 76.6 %reduce-scatter.2.cloned.1.call-done = f32[32,1056]{1,0:T(8,128)} async-done(((f32[512,1056]{1,0:T(8,128)}), f32[32,1056]{1,0:T(8,128)}) %reduce-scatter.2.cloned.1.call-update) | async-done | bytes 135184 | tf_op jit(solution)/shard_map/reduce_scatter | solution.py:38
  457.3 0.9 split.88
  458.2 0.8 reshape.77
  459.0 1.6 convolution_add_fusion.1
  (55 shorter events, 5.4 us)
Async XLA Ops:
  11.1 79.5 %all-to-all-start = ((f32[16,32,4,1,256]{4,3,2,1,0:T(1,128)}), f32[16,32,4,1,256]{4,3,2,1,0:T(1,128)S(1)}, u32[]{:S(2)}, u32[]{:S(2)}) async-start(f32[16,32,4,1,256]{4,3,2,1,0:T(1,128)} %broadcast_in_dim.4), calls=%async_computation | async-start | bytes 4194304 | tf_op jit(solution)/shard_map/all_to_all | solution.py:9
  18.5 198.7 %all-gather.3.cloned.1.call-start = ((), (), s32[]{:S(2)}) async-start(), calls=%async_computation.5 | async-start | bytes 2228224 | tf_op jit(solution)/shard_map/all_gather | solution.py:88
  100.0 4.1 copy-start
  169.9 146.5 %all-gather.5.cloned.1.call-start = ((), (), s32[]{:S(2)}) async-start(), calls=%async_computation.6 | async-start | bytes 2785280 | tf_op jit(solution)/shard_map/all_gather | solution.py:92
  207.3 9.2 %copy-start.4 = (f32[32,6,1,256]{3,2,1,0:T(1,128)S(1)}, f32[32,6,1,256]{3,2,1,0:T(1,128)}, u32[]{:S(2)}) copy-start(f32[32,6,1,256]{3,2,1,0:T(1,128)} %param.9) | copy-start | bytes 589828
  217.2 13.7 %copy-start.2 = (f32[512,512]{1,0:T(8,128)}, f32[512,512]{1,0:T(8,128)S(1)}, u32[]{:S(2)}) copy-start(f32[512,512]{1,0:T(8,128)S(1)} %select_maximum_fusion) | copy-start | bytes 3145732
  279.8 177.5 %reduce-scatter.2.cloned.1.call-start = ((), (), s32[]{:S(2)}) async-start(), calls=%async_computation.7 | async-start | bytes 2506752 | tf_op jit(solution)/shard_map/reduce_scatter | solution.py:38
  366.4 2.8 copy-start.1
  369.2 7.2 %copy-start.3 = (f32[32,1024]{1,0:T(8,128)S(1)}, f32[32,1024]{1,0:T(8,128)}, u32[]{:S(2)}) copy-start(f32[32,1024]{1,0:T(8,128)} %reduce_sum.18) | copy-start | bytes 393220
Sparse Core Ops, SparseCore 0:
  170.0 37.7 all-gather.2
  279.9 36.4 all-gather.4
  379.9 77.3 reduce-scatter.1
